TPU v7x, 32 devices: a whole 2x2x4 slice. The times are simulated.
32 devices in a mesh: groups: 2 (over y), ctx: 4 (over z), head: 2 (over x), rep: 2 (over core).
Axes of the slice: x: 2, y: 2, z: 4, core: 2. Of those that a mesh axis runs over, the one named last changes fastest.
Arguments:
- queries: bfloat16 [2048, 4096], P(('groups', 'ctx'), ('head', 'rep')), parts along dimension 0, may hold values from -24 to 24
- keys: bfloat16 [2048, 1024], P(('groups', 'ctx'), ('head', 'rep')), parts along dimension 0, may hold values from -6 to 6
- values: bfloat16 [2048, 1024], P(('groups', 'ctx'), ('head', 'rep')), parts along dimension 0, may hold values from -6 to 6
- span_order: int32 [8], replicated, may hold values from 0 to 7, as said below
Outputs:
- attended: bfloat16 [2048, 4096], P(('groups', 'ctx'), ('head', 'rep')), parts along dimension 0
There are 2 independent parts, one for each index of `groups`. A program takes and returns all parts, laid end to end along the dimension named above; an argument that names none is the same for every part. Nothing has to cross between parts.
Inputs may be any that keep to these rules, and one draw needn't show every extreme that they name: `span_order`: A permutation of the spans in which entries 2 d and 2 d + 1 are c and 7 - c for some c.
All inputs are finite; a program needn't handle non-finite values.
Results may differ from a plain program's by a relative error of at most 0.0047.
Values may be sent and summed in bfloat16 or wider, within the bound.
A program may use at most 64 MiB of HBM per device.

v0:
```python
import math
import jax
import jax.numpy as jnp
from jax import lax
from jax.sharding import PartitionSpec as P

HEAD_SIZE = 128
masked_score = -1e30


def lookup_positions(span_order, first_row, row_count, span_rows):
    row_ids = first_row + jnp.arange(row_count, dtype=jnp.int32)
    span_ids = row_ids // span_rows
    span_table = jnp.arange(span_order.shape[0], dtype=jnp.int32)
    span_starts = jnp.sum(
        jnp.where(span_ids[:, None] == span_table[None, :], span_order[None, :], 0), axis=1
    )
    return span_starts * span_rows + row_ids % span_rows


def source_partials(query_block, query_pos, key_group, value_group, key_pos, head_dim):
    score_scale = 1.0 / math.sqrt(head_dim)
    scores = (
        jnp.einsum("rhgd,cshd->crhgs", query_block, key_group, preferred_element_type=jnp.float32)
        * score_scale
    )
    allowed = (key_pos[:, None, :] <= query_pos[None, :, None])[:, :, None, None, :]
    masked = jnp.where(allowed, scores, masked_score)
    row_top = jnp.max(masked, axis=-1)
    weights = jnp.where(allowed, jnp.exp(masked - row_top[..., None]), 0.0)
    row_total = jnp.sum(weights, axis=-1)
    numerator = jnp.einsum(
        "crhgs,cshd->crhgd",
        weights.astype(jnp.bfloat16),
        value_group,
        preferred_element_type=jnp.float32,
    )
    partial_value = (numerator / jnp.maximum(row_total, 1.0)[..., None]).astype(jnp.bfloat16)
    return (partial_value, row_top, row_total)


def absorb(running, partial_value, row_top, row_total):
    run_top, run_total, run_sum = running
    new_top = jnp.maximum(run_top, row_top)
    rescale = jnp.exp(run_top - new_top)
    source_weight = row_total * jnp.exp(row_top - new_top)
    return (
        new_top,
        run_total * rescale + source_weight,
        run_sum * rescale[..., None] + source_weight[..., None] * partial_value.astype(jnp.float32),
    )


def shards(queries, keys, values, span_order):
    rows_here = queries.shape[0]
    span_rows = rows_here // 2
    head_dim = HEAD_SIZE
    kv_heads = keys.shape[1] // head_dim
    common_values = queries.shape[1] // keys.shape[1]
    my_index = lax.axis_index("ctx")
    own_pos = lookup_positions(span_order, my_index * rows_here, rows_here, span_rows)
    q_local = queries.reshape(rows_here, kv_heads, common_values, head_dim)
    initial = (
        jnp.full((rows_here, kv_heads, common_values), masked_score, jnp.float32),
        jnp.zeros((rows_here, kv_heads, common_values), jnp.float32),
        jnp.zeros((rows_here, kv_heads, common_values, head_dim), jnp.float32),
    )
    running = initial
    k_piece = lax.all_gather(keys, "ctx", axis=0, tiled=True)
    v_piece = lax.all_gather(values, "ctx", axis=0, tiled=True)
    shard_count = k_piece.shape[0] // rows_here
    per_turn = 2
    turn_count = shard_count // per_turn
    k_pos = lookup_positions(span_order, jnp.int32(0), k_piece.shape[0], span_rows)
    k_steps = k_piece.reshape(turn_count, per_turn, rows_here, kv_heads, head_dim)
    v_steps = v_piece.reshape(turn_count, per_turn, rows_here, kv_heads, head_dim)
    p_steps = k_pos.reshape(turn_count, per_turn, rows_here)

    def one_turn(carried, inputs_now):
        partial_value, row_top, row_total = source_partials(
            q_local, own_pos, inputs_now[0], inputs_now[1], inputs_now[2], head_dim
        )
        for member in range(per_turn):
            carried = absorb(carried, partial_value[member], row_top[member], row_total[member])
        return (carried, None)

    running, unused = lax.scan(one_turn, running, (k_steps, v_steps, p_steps))
    merged = running[2] / running[1][..., None]
    return merged.reshape(rows_here, kv_heads * common_values * head_dim).astype(jnp.bfloat16)


def solution(mesh):
    return jax.shard_map(
        shards,
        mesh=mesh,
        in_specs=(
            P(("groups", "ctx"), ("head", "rep")),
            P(("groups", "ctx"), ("head", "rep")),
            P(("groups", "ctx"), ("head", "rep")),
            P(),
        ),
        out_specs=P(("groups", "ctx"), ("head", "rep")),
        check_vma=False,
    )
```

profile of v0, /device:TPU:0, one launch (start us, length us, event | category | flops | bytes accessed | tf_op | source)
XLA Modules:
  0.0 60.6 jit_solution(10825627206917604020)
XLA Ops:
  0.0 0.8 %select_reduce_fusion.1 = s32[256]{0:T(256)S(1)} fusion(s32[8]{0:T(128)} %param.9, s32[256]{0:T(256)S(1)} %and_select_fusion.2), kind=kLoop, calls=%fused_computation.45 | loop fusion | flops 5888 | bytes 2080 | tf_op jit(solution)/shard_map/reduce_sum | solution.py:15
  0.8 1.2 %copy.30 = bf16[256,1024]{0,1:T(8,128)(2,1)S(1)} copy(bf16[256,1024]{1,0:T(8,128)(2,1)} %param.6) | data formatting | bytes 1048576 | tf_op args[0]
  2.1 1.0 %copy.32 = bf16[256,2,4,128]{3,0,2,1:T(8,128)(2,1)} copy(bf16[256,2,4,128]{0,3,2,1:T(8,128)(2,1)S(1)} %bitcast.99) | data formatting | bytes 1048576
  3.1 17.6 %all_gather.6 = bf16[1024,256]{1,0:T(8,128)(2,1)S(1)} all-gather(bf16[256,256]{1,0:T(8,128)(2,1)} %param.7), channel_id=1, replica_groups=mesh['groups'=2,'ctx'=4,'head'=2,'rep'=2] {'ctx'}, dimensions={0}, use_global_device_ids=true | all-gather | bytes 655360 | tf_op jit(solution)/shard_map/all_gather | solution.py:69
  20.7 0.9 %reshape.66 = bf16[2,2,256,2,128]{4,3,2,1,0:T(2,128)(2,1)} reshape(bf16[1024,256]{1,0:T(8,128)(2,1)S(1)} %all_gather.6) | data formatting | bytes 1048576 | tf_op jit(solution)/shard_map/reshape | solution.py:75
  21.6 16.6 %all_gather.7 = bf16[1024,256]{1,0:T(8,128)(2,1)S(1)} all-gather(bf16[256,256]{1,0:T(8,128)(2,1)} %param.8), channel_id=1, replica_groups=mesh['groups'=2,'ctx'=4,'head'=2,'rep'=2] {'ctx'}, dimensions={0}, use_global_device_ids=true | all-gather | bytes 655360 | tf_op jit(solution)/shard_map/all_gather | solution.py:70
  38.2 0.9 %reshape.68 = bf16[2,2,256,2,128]{4,3,2,1,0:T(2,128)(2,1)} reshape(bf16[1024,256]{1,0:T(8,128)(2,1)S(1)} %all_gather.7) | data formatting | bytes 1048576 | tf_op jit(solution)/shard_map/reshape | solution.py:76
  39.3 20.2 %while.15 = (s32[]{:T(128)}, f32[256,2,4]{0,2,1:T(4,128)S(1)}, f32[256,2,4]{0,2,1:T(4,128)S(1)}, f32[256,2,4,128]{0,3,2,1:T(8,128)S(1)}, s32[2,2,256]{2,1,0:T(2,...) while((s32[]{:T(128)}, f32[256,2,4]{0,2,1:T(4,128)S(1)}, ...), condition=%wide.region_5.6_spmd.clone, body=%wide.region_2.5_spmd.clone.sunk | while | flops 549871616 | bytes 19995776 | solution.py:87
  39.3 1.4 %constant_dynamic-slice_fusion.3 = (bf16[1,2,256,2,128]{4,3,2,1,0:T(2,128)(2,1)S(1)}, bf16[1,2,256,2,128]{4,3,2,1,0:T(2,128)(2,1)S(1)}) fusion(bf16[2,2,256,2,128]{4,3,2,1,0:T(2,128)(2,1)} %get-tuple-element.251, s32[]{:T(128)} %get-tuple-element.232, bf16[2,2,256,2,128]{4,3,2,1,0:T(2,128)(2,1)} %get-tuple-element.249), kind=kLoop, calls=%fused_computation.38.clone.1 | loop fusion | bytes 1048580 | tf_op jit(solution)/shard_map/while/body/jit(dynamic_index_in_dim)/dynamic_slice | solution.py:87
  40.7 0.1 broadcast_compare_fusion.3
  40.8 1.9 %fusion.43 = (f32[2,256,2,4]{1,3,0,2:T(4,128)S(1)}, f32[2,2,256,256,4]{3,2,4,1,0:T(8,128)S(1)}) fusion(pred[2,256,256]{1,2,0:T(8,128)(4,1)S(1)} %broadcast_compare_fusion.3, bf16[256,2,4,128]{3,0,2,1:T(8,128)(2,1)} %get-tuple-element.250, bf16[1,2,256,2,128]{4,3,2,1,0:T(2,128)(2,1)S(1)} %get-tuple-element.209), kind=kOutput, calls=%fused_computation.2.clone.1 | convolution fusion | flops 271577088 | bytes 5128192 | tf_op jit(solution)/shard_map/while/body/eval_jaxpr/rhgd,cshd->crhgs/dot_general | solution.py:24
  42.7 1.2 %fusion.44 = (bf16[2,256,2,4,256]{1,4,3,0,2:T(8,128)(2,1)S(1)}, f32[2,256,2,4]{1,3,0,2:T(4,128)S(1)}) fusion(f32[2,2,256,256,4]{3,2,4,1,0:T(8,128)S(1)} %get-tuple-element.211, f32[2,256,2,4]{1,3,0,2:T(4,128)S(1)} %get-tuple-element.210, pred[2,256,256]{1,2,0:T(8,128)(4,1)S(1)} %broadcast_compare_fusion.3), kind=kLoop, calls=%fused_computation.3.clone.1 | loop fusion | flops 6287360 | bytes 6455296 | tf_op jit(solution)/shard_map/while/body/eval_jaxpr/convert_element_type | solution.py:34
  43.9 0.9 %copy.63 = bf16[1,2,256,2,128]{2,4,3,1,0:T(8,128)(2,1)} copy(bf16[1,2,256,2,128]{4,3,2,1,0:T(2,128)(2,1)S(1)} %get-tuple-element.216) | data formatting | bytes 524288 | tf_op jit(solution)/shard_map/while/body/jit(dynamic_index_in_dim)/dynamic_slice | solution.py:87
  44.8 2.4 %fusion.46 = bf16[2,256,2,4,128]{1,4,3,2,0:T(8,128)(2,1)} fusion(bf16[2,256,2,4,256]{1,4,3,0,2:T(8,128)(2,1)S(1)} %get-tuple-element.215, bf16[1,2,256,2,128]{2,4,3,1,0:T(8,128)(2,1)} %copy.63, f32[2,256,2,4]{1,3,0,2:T(4,128)S(1)} %get-tuple-element.212), kind=kOutput, calls=%fused_computation.6.clone.1 | convolution fusion | flops 269488128 | bytes 3424256 | tf_op jit(solution)/shard_map/while/body/eval_jaxpr/crhgs,cshd->crhgd/dot_general | solution.py:32
  47.2 2.1 %fusion.47 = f32[256,2,4,128]{0,3,2,1:T(8,128)S(1)} fusion(f32[256,2,4,128]{0,3,2,1:T(8,128)S(1)} %get-tuple-element.235, bf16[2,256,2,4,128]{1,4,3,2,0:T(8,128)(2,1)} %fusion.46, f32[256,2,4]{0,2,1:T(4,128)S(1)} %get-tuple-element.217, f32[256,2,4]{0,2,1:T(4,128)S(1)} %get-tuple-element.218, f32[256,2,4]{0,2,1:T(4,128)S(1)} %get-tuple-element.219, ...), kind=kLoop, calls=%fused_computation.10.clone.1 | loop fusion | flops 2359296 | bytes 3178497 | tf_op jit(solution)/shard_map/while/body/eval_jaxpr/add | solution.py:50
  49.4 1.4 %constant_dynamic-slice_fusion.3 = (bf16[1,2,256,2,128]{4,3,2,1,0:T(2,128)(2,1)S(1)}, bf16[1,2,256,2,128]{4,3,2,1,0:T(2,128)(2,1)S(1)}) fusion(bf16[2,2,256,2,128]{4,3,2,1,0:T(2,128)(2,1)} %get-tuple-element.251, s32[]{:T(128)} %get-tuple-element.232, bf16[2,2,256,2,128]{4,3,2,1,0:T(2,128)(2,1)} %get-tuple-element.249), kind=kLoop, calls=%fused_computation.38.clone.1 | loop fusion | bytes 1048580 | tf_op jit(solution)/shard_map/while/body/jit(dynamic_index_in_dim)/dynamic_slice | solution.py:87
  50.8 0.1 broadcast_compare_fusion.3
  50.9 1.9 %fusion.43 = (f32[2,256,2,4]{1,3,0,2:T(4,128)S(1)}, f32[2,2,256,256,4]{3,2,4,1,0:T(8,128)S(1)}) fusion(pred[2,256,256]{1,2,0:T(8,128)(4,1)S(1)} %broadcast_compare_fusion.3, bf16[256,2,4,128]{3,0,2,1:T(8,128)(2,1)} %get-tuple-element.250, bf16[1,2,256,2,128]{4,3,2,1,0:T(2,128)(2,1)S(1)} %get-tuple-element.209), kind=kOutput, calls=%fused_computation.2.clone.1 | convolution fusion | flops 271577088 | bytes 5128192 | tf_op jit(solution)/shard_map/while/body/eval_jaxpr/rhgd,cshd->crhgs/dot_general | solution.py:24
  52.8 1.2 %fusion.44 = (bf16[2,256,2,4,256]{1,4,3,0,2:T(8,128)(2,1)S(1)}, f32[2,256,2,4]{1,3,0,2:T(4,128)S(1)}) fusion(f32[2,2,256,256,4]{3,2,4,1,0:T(8,128)S(1)} %get-tuple-element.211, f32[2,256,2,4]{1,3,0,2:T(4,128)S(1)} %get-tuple-element.210, pred[2,256,256]{1,2,0:T(8,128)(4,1)S(1)} %broadcast_compare_fusion.3), kind=kLoop, calls=%fused_computation.3.clone.1 | loop fusion | flops 6287360 | bytes 6455296 | tf_op jit(solution)/shard_map/while/body/eval_jaxpr/convert_element_type | solution.py:34
  54.0 0.9 %copy.63 = bf16[1,2,256,2,128]{2,4,3,1,0:T(8,128)(2,1)} copy(bf16[1,2,256,2,128]{4,3,2,1,0:T(2,128)(2,1)S(1)} %get-tuple-element.216) | data formatting | bytes 524288 | tf_op jit(solution)/shard_map/while/body/jit(dynamic_index_in_dim)/dynamic_slice | solution.py:87
  54.9 2.4 %fusion.46 = bf16[2,256,2,4,128]{1,4,3,2,0:T(8,128)(2,1)} fusion(bf16[2,256,2,4,256]{1,4,3,0,2:T(8,128)(2,1)S(1)} %get-tuple-element.215, bf16[1,2,256,2,128]{2,4,3,1,0:T(8,128)(2,1)} %copy.63, f32[2,256,2,4]{1,3,0,2:T(4,128)S(1)} %get-tuple-element.212), kind=kOutput, calls=%fused_computation.6.clone.1 | convolution fusion | flops 269488128 | bytes 3424256 | tf_op jit(solution)/shard_map/while/body/eval_jaxpr/crhgs,cshd->crhgd/dot_general | solution.py:32
  57.3 2.1 %fusion.47 = f32[256,2,4,128]{0,3,2,1:T(8,128)S(1)} fusion(f32[256,2,4,128]{0,3,2,1:T(8,128)S(1)} %get-tuple-element.235, bf16[2,256,2,4,128]{1,4,3,2,0:T(8,128)(2,1)} %fusion.46, f32[256,2,4]{0,2,1:T(4,128)S(1)} %get-tuple-element.217, f32[256,2,4]{0,2,1:T(4,128)S(1)} %get-tuple-element.218, f32[256,2,4]{0,2,1:T(4,128)S(1)} %get-tuple-element.219, ...), kind=kLoop, calls=%fused_computation.10.clone.1 | loop fusion | flops 2359296 | bytes 3178497 | tf_op jit(solution)/shard_map/while/body/eval_jaxpr/add | solution.py:50
  59.5 0.1 divide_convert_fusion
  59.6 1.0 %copy.39 = bf16[256,1024]{1,0:T(8,128)(2,1)} copy(bf16[256,1024]{0,1:T(8,128)(2,1)S(1)} %bitcast.98) | data formatting | bytes 1048576 | tf_op jit(solution)/shard_map/convert_element_type | solution.py:89
  (16 shorter events, 0.2 us)
Async XLA Ops:
  0.0 39.1 %copy-start = (s32[8]{0:T(128)S(1)}, s32[8]{0:T(128)}, u32[]{:S(2)}) copy-start(s32[8]{0:T(128)} %param.9) | copy-start | bytes 100
where the time goes:
time: 61 us; the launch traced here: 60.6 us
  blocking collectives  34.1 us (56%)
  local copies, waits for them, and re-layouts  9.69 us (16%)
  matrix products  8.65 us (14%)
  other arithmetic  7.94 us (13%)
    all_gather x1, blocking collectives, shards(): k_piece = lax.all_gather(keys, 'ctx', axis=0, tiled=True)  17.6 us
    all_gather x1, blocking collectives, shards(): v_piece = lax.all_gather(values, 'ctx', axis=0, tiled=True)  16.6 us
    dot_general x2, matrix products, source_partials(): jnp.einsum('crhgs,cshd->crhgd', weights.astype(jnp.bfloat16), value_group...  4.85 us
    dynamic_slice x4, local copies, waits for them, and re-layouts, shards(): running, unused = lax.scan(one_turn, running, (k_steps, v_steps, p_steps))  4.53 us
    add x2, other arithmetic, absorb(): run_sum * rescale[..., None]  4.23 us
    dot_general x2, matrix products, source_partials(): jnp.einsum('rhgd,cshd->crhgs', query_block, key_group, preferred_element_...  3.8 us
    convert_element_type x2, other arithmetic, source_partials(): weights.astype(jnp.bfloat16)  2.34 us
    unnamed x4, local copies, waits for them, and re-layouts  2.27 us

commit v1 on v0

--- a/solution.py
+++ b/solution.py
@@ -66,7 +66,12 @@
         jnp.zeros((rows_here, kv_heads, common_values, head_dim), jnp.float32),
     )
     running = initial
-    k_piece = lax.all_gather(keys, "ctx", axis=0, tiled=True)
+    ring = [keys]
+    for hop in range(3):
+        ring.append(lax.ppermute(ring[-1], "ctx", [(dev, (dev + 1) % 4) for dev in range(4)]))
+    k_piece = jnp.roll(
+        jnp.concatenate(ring[::-1], axis=0), (lax.axis_index("ctx") + 1) * ring[0].shape[0], axis=0
+    )
     v_piece = lax.all_gather(values, "ctx", axis=0, tiled=True)
     shard_count = k_piece.shape[0] // rows_here
     per_turn = 2

time: 61 us -> 56.3 us (0.923)
  blocking collectives: 34.1 us -> 16.1 us
  waiting for transfers between devices: 0 us -> 9.49 us
  starting transfers between devices: 0 us -> 3.06 us
    all_gather x1 -> x0, blocking collectives: 17.6 us -> none  [shards(): k_piece = lax.all_gather(keys, 'ctx', axis=0, tiled=True)]
    ppermute x0 -> x3, waiting for transfers between devices: none -> 9.49 us  [shards(): lax.ppermute(ring[-1], 'ctx', [(dev, (dev + 1) % 4) for dev in range(4)])]
    ppermute x0 -> x3, starting transfers between devices: none -> 3.06 us  [shards(): lax.ppermute(ring[-1], 'ctx', [(dev, (dev + 1) % 4) for dev in range(4)])]
    unnamed x4 -> x11, local copies, waits for them, and re-layouts: 2.27 us -> 2.35 us
  transfers between devices with their start and end apart: 0 -> 3, of which waited for: 0 -> 2; matrix products, arithmetic and copies ran while one was open for 0% -> 8% of each run, Pallas kernels for 0% -> 0%
where the time goes in v1:
time: 56.3 us; the launch traced here: 55.9 us
  blocking collectives  16.1 us (29%)
  local copies, waits for them, and re-layouts  9.82 us (17%)
  waiting for transfers between devices  9.49 us (17%)
  matrix products  8.64 us (15%)
  other arithmetic  8.54 us (15%)
  starting transfers between devices  3.06 us (5%)
    all_gather x1, blocking collectives, shards(): v_piece = lax.all_gather(values, 'ctx', axis=0, tiled=True)  16.1 us
    ppermute x3, waiting for transfers between devices, shards(): lax.ppermute(ring[-1], 'ctx', [(dev, (dev + 1) % 4) for dev in range(4)])  9.49 us
    dot_general x2, matrix products, source_partials(): jnp.einsum('crhgs,cshd->crhgd', weights.astype(jnp.bfloat16), value_group...  4.85 us
    dynamic_slice x4, local copies, waits for them, and re-layouts, shards(): running, unused = lax.scan(one_turn, running, (k_steps, v_steps, p_steps))  4.53 us
    add x2, other arithmetic, absorb(): run_sum * rescale[..., None]  4.23 us
    dot_general x2, matrix products, source_partials(): jnp.einsum('rhgd,cshd->crhgs', query_block, key_group, preferred_element_...  3.8 us
    ppermute x3, starting transfers between devices, shards(): lax.ppermute(ring[-1], 'ctx', [(dev, (dev + 1) % 4) for dev in range(4)])  3.06 us
    unnamed x11, local copies, waits for them, and re-layouts  2.35 us
  transfers between devices with their start and end apart: 3, of which 2 were waited for; matrix products, arithmetic and copies ran while one was open for 8% of the time, Pallas kernels for 0%

profile of v1, /device:TPU:0, one launch (start us, length us, event | category | flops | bytes accessed | tf_op | source)
XLA Modules:
  0.0 55.9 jit_solution(14362548944117663367)
XLA Ops:
  0.0 3.1 %collective-permute-start = (bf16[256,256]{1,0:T(8,128)(2,1)}, bf16[256,256]{1,0:T(8,128)(2,1)S(1)}, u32[]{:S(2)}, u32[]{:S(2)}) collective-permute-start(bf16[256,256]{1,0:T(8,128)(2,1)} %param.7), channel_id=1, source_target_pairs={{0,4},{4,8},{8,12},{12,0},{1,5},{5,9},{9,13},{13,1},{2,6},{6,10},{... | collective-permute-start | bytes 393224 | tf_op jit(solution)/shard_map/ppermute | solution.py:71
  3.1 0.7 %select_reduce_fusion = s32[1024]{0:T(1024)S(1)} fusion(s32[8]{0:T(128)} %param.9, s32[1024]{0:T(1024)S(1)} %add_select_fusion), kind=kLoop, calls=%fused_computation.41 | loop fusion | flops 23552 | bytes 8224 | tf_op jit(solution)/shard_map/reduce_sum | solution.py:15
  3.8 16.1 %all_gather.3 = bf16[1024,256]{1,0:T(8,128)(2,1)S(1)} all-gather(bf16[256,256]{1,0:T(8,128)(2,1)} %param.8), channel_id=1, replica_groups=mesh['groups'=2,'ctx'=4,'head'=2,'rep'=2] {'ctx'}, dimensions={0}, use_global_device_ids=true | all-gather | bytes 655360 | tf_op jit(solution)/shard_map/all_gather | solution.py:75
  20.0 1.2 %copy.30 = bf16[256,1024]{0,1:T(8,128)(2,1)S(1)} copy(bf16[256,1024]{1,0:T(8,128)(2,1)} %param.6) | data formatting | bytes 1048576 | tf_op args[0]
  21.2 1.0 %copy.32 = bf16[256,2,4,128]{3,0,2,1:T(8,128)(2,1)} copy(bf16[256,2,4,128]{0,3,2,1:T(8,128)(2,1)S(1)} %bitcast.99) | data formatting | bytes 1048576
  22.3 0.9 %reshape.68 = bf16[2,2,256,2,128]{4,3,2,1,0:T(2,128)(2,1)} reshape(bf16[1024,256]{1,0:T(8,128)(2,1)S(1)} %all_gather.3) | data formatting | bytes 1048576 | tf_op jit(solution)/shard_map/reshape | solution.py:81
  23.2 0.7 %select_reduce_fusion.1 = s32[256]{0:T(256)S(1)} fusion(s32[8]{0:T(128)} %param.9, s32[256]{0:T(256)S(1)} %and_select_fusion.2), kind=kLoop, calls=%fused_computation.53 | loop fusion | flops 5888 | bytes 2080 | tf_op jit(solution)/shard_map/reduce_sum | solution.py:15
  23.9 2.7 %collective-permute-done.1 = bf16[256,256]{1,0:T(8,128)(2,1)S(1)} collective-permute-done((bf16[256,256]{1,0:T(8,128)(2,1)S(1)}, bf16[256,256]{1,0:T(8,128)(2,1)S(1)}, u32[]{:S(2)}, u32[]{:S(2)}) %collective-permute-start.1) | collective-permute-done | bytes 131104 | tf_op jit(solution)/shard_map/ppermute | solution.py:71
  26.7 6.8 %collective-permute-done.2 = bf16[256,256]{1,0:T(8,128)(2,1)S(1)} collective-permute-done((bf16[256,256]{1,0:T(8,128)(2,1)S(1)}, bf16[256,256]{1,0:T(8,128)(2,1)S(1)}, u32[]{:S(2)}, u32[]{:S(2)}) %collective-permute-start.2) | collective-permute-done | bytes 131104 | tf_op jit(solution)/shard_map/ppermute | solution.py:71
  33.6 0.9 %reshape.66 = bf16[2,2,256,2,128]{4,3,2,1,0:T(2,128)(2,1)} reshape(bf16[1024,256]{1,0:T(8,128)(2,1)S(1)} %constant_dynamic-slice_fusion.2) | data formatting | bytes 1048576 | tf_op jit(solution)/shard_map/reshape | solution.py:80
  34.6 20.2 %while.15 = (s32[]{:T(128)}, f32[256,2,4]{0,2,1:T(4,128)S(1)}, f32[256,2,4]{0,2,1:T(4,128)S(1)}, f32[256,2,4,128]{0,3,2,1:T(8,128)S(1)}, s32[2,2,256]{2,1,0:T(2,...) while((s32[]{:T(128)}, f32[256,2,4]{0,2,1:T(4,128)S(1)}, ...), condition=%wide.region_5.6_spmd.clone, body=%wide.region_2.5_spmd.clone.sunk | while | flops 549871616 | bytes 19995776 | solution.py:92
  34.6 1.4 %constant_dynamic-slice_fusion.4 = (bf16[1,2,256,2,128]{4,3,2,1,0:T(2,128)(2,1)S(1)}, bf16[1,2,256,2,128]{4,3,2,1,0:T(2,128)(2,1)S(1)}) fusion(bf16[2,2,256,2,128]{4,3,2,1,0:T(2,128)(2,1)} %get-tuple-element.251, s32[]{:T(128)} %get-tuple-element.232, bf16[2,2,256,2,128]{4,3,2,1,0:T(2,128)(2,1)} %get-tuple-element.249), kind=kLoop, calls=%fused_computation.38.clone.1 | loop fusion | bytes 1048580 | tf_op jit(solution)/shard_map/while/body/jit(dynamic_index_in_dim)/dynamic_slice | solution.py:92
  36.1 1.9 %fusion.43 = (f32[2,256,2,4]{1,3,0,2:T(4,128)S(1)}, f32[2,2,256,256,4]{3,2,4,1,0:T(8,128)S(1)}) fusion(pred[2,256,256]{1,2,0:T(8,128)(4,1)S(1)} %broadcast_compare_fusion.3, bf16[256,2,4,128]{3,0,2,1:T(8,128)(2,1)} %get-tuple-element.250, bf16[1,2,256,2,128]{4,3,2,1,0:T(2,128)(2,1)S(1)} %get-tuple-element.209), kind=kOutput, calls=%fused_computation.2.clone.1 | convolution fusion | flops 271577088 | bytes 5128192 | tf_op jit(solution)/shard_map/while/body/eval_jaxpr/rhgd,cshd->crhgs/dot_general | solution.py:24
  38.0 1.2 %fusion.44 = (bf16[2,256,2,4,256]{1,4,3,0,2:T(8,128)(2,1)S(1)}, f32[2,256,2,4]{1,3,0,2:T(4,128)S(1)}) fusion(f32[2,2,256,256,4]{3,2,4,1,0:T(8,128)S(1)} %get-tuple-element.211, f32[2,256,2,4]{1,3,0,2:T(4,128)S(1)} %get-tuple-element.210, pred[2,256,256]{1,2,0:T(8,128)(4,1)S(1)} %broadcast_compare_fusion.3), kind=kLoop, calls=%fused_computation.3.clone.1 | loop fusion | flops 6287360 | bytes 6455296 | tf_op jit(solution)/shard_map/while/body/eval_jaxpr/convert_element_type | solution.py:34
  39.2 0.9 %copy.63 = bf16[1,2,256,2,128]{2,4,3,1,0:T(8,128)(2,1)} copy(bf16[1,2,256,2,128]{4,3,2,1,0:T(2,128)(2,1)S(1)} %get-tuple-element.216) | data formatting | bytes 524288 | tf_op jit(solution)/shard_map/while/body/jit(dynamic_index_in_dim)/dynamic_slice | solution.py:92
  40.1 2.4 %fusion.46 = bf16[2,256,2,4,128]{1,4,3,2,0:T(8,128)(2,1)} fusion(bf16[2,256,2,4,256]{1,4,3,0,2:T(8,128)(2,1)S(1)} %get-tuple-element.215, bf16[1,2,256,2,128]{2,4,3,1,0:T(8,128)(2,1)} %copy.63, f32[2,256,2,4]{1,3,0,2:T(4,128)S(1)} %get-tuple-element.212), kind=kOutput, calls=%fused_computation.6.clone.1 | convolution fusion | flops 269488128 | bytes 3424256 | tf_op jit(solution)/shard_map/while/body/eval_jaxpr/crhgs,cshd->crhgd/dot_general | solution.py:32
  42.5 2.1 %fusion.47 = f32[256,2,4,128]{0,3,2,1:T(8,128)S(1)} fusion(f32[256,2,4,128]{0,3,2,1:T(8,128)S(1)} %get-tuple-element.235, bf16[2,256,2,4,128]{1,4,3,2,0:T(8,128)(2,1)} %fusion.46, f32[256,2,4]{0,2,1:T(4,128)S(1)} %get-tuple-element.217, f32[256,2,4]{0,2,1:T(4,128)S(1)} %get-tuple-element.218, f32[256,2,4]{0,2,1:T(4,128)S(1)} %get-tuple-element.219, ...), kind=kLoop, calls=%fused_computation.10.clone.1 | loop fusion | flops 2359296 | bytes 3178497 | tf_op jit(solution)/shard_map/while/body/eval_jaxpr/add | solution.py:50
  44.6 1.4 %constant_dynamic-slice_fusion.4 = (bf16[1,2,256,2,128]{4,3,2,1,0:T(2,128)(2,1)S(1)}, bf16[1,2,256,2,128]{4,3,2,1,0:T(2,128)(2,1)S(1)}) fusion(bf16[2,2,256,2,128]{4,3,2,1,0:T(2,128)(2,1)} %get-tuple-element.251, s32[]{:T(128)} %get-tuple-element.232, bf16[2,2,256,2,128]{4,3,2,1,0:T(2,128)(2,1)} %get-tuple-element.249), kind=kLoop, calls=%fused_computation.38.clone.1 | loop fusion | bytes 1048580 | tf_op jit(solution)/shard_map/while/body/jit(dynamic_index_in_dim)/dynamic_slice | solution.py:92
  46.2 1.9 %fusion.43 = (f32[2,256,2,4]{1,3,0,2:T(4,128)S(1)}, f32[2,2,256,256,4]{3,2,4,1,0:T(8,128)S(1)}) fusion(pred[2,256,256]{1,2,0:T(8,128)(4,1)S(1)} %broadcast_compare_fusion.3, bf16[256,2,4,128]{3,0,2,1:T(8,128)(2,1)} %get-tuple-element.250, bf16[1,2,256,2,128]{4,3,2,1,0:T(2,128)(2,1)S(1)} %get-tuple-element.209), kind=kOutput, calls=%fused_computation.2.clone.1 | convolution fusion | flops 271577088 | bytes 5128192 | tf_op jit(solution)/shard_map/while/body/eval_jaxpr/rhgd,cshd->crhgs/dot_general | solution.py:24
  48.1 1.2 %fusion.44 = (bf16[2,256,2,4,256]{1,4,3,0,2:T(8,128)(2,1)S(1)}, f32[2,256,2,4]{1,3,0,2:T(4,128)S(1)}) fusion(f32[2,2,256,256,4]{3,2,4,1,0:T(8,128)S(1)} %get-tuple-element.211, f32[2,256,2,4]{1,3,0,2:T(4,128)S(1)} %get-tuple-element.210, pred[2,256,256]{1,2,0:T(8,128)(4,1)S(1)} %broadcast_compare_fusion.3), kind=kLoop, calls=%fused_computation.3.clone.1 | loop fusion | flops 6287360 | bytes 6455296 | tf_op jit(solution)/shard_map/while/body/eval_jaxpr/convert_element_type | solution.py:34
  49.3 0.9 %copy.63 = bf16[1,2,256,2,128]{2,4,3,1,0:T(8,128)(2,1)} copy(bf16[1,2,256,2,128]{4,3,2,1,0:T(2,128)(2,1)S(1)} %get-tuple-element.216) | data formatting | bytes 524288 | tf_op jit(solution)/shard_map/while/body/jit(dynamic_index_in_dim)/dynamic_slice | solution.py:92
  50.2 2.4 %fusion.46 = bf16[2,256,2,4,128]{1,4,3,2,0:T(8,128)(2,1)} fusion(bf16[2,256,2,4,256]{1,4,3,0,2:T(8,128)(2,1)S(1)} %get-tuple-element.215, bf16[1,2,256,2,128]{2,4,3,1,0:T(8,128)(2,1)} %copy.63, f32[2,256,2,4]{1,3,0,2:T(4,128)S(1)} %get-tuple-element.212), kind=kOutput, calls=%fused_computation.6.clone.1 | convolution fusion | flops 269488128 | bytes 3424256 | tf_op jit(solution)/shard_map/while/body/eval_jaxpr/crhgs,cshd->crhgd/dot_general | solution.py:32
  52.6 2.1 %fusion.47 = f32[256,2,4,128]{0,3,2,1:T(8,128)S(1)} fusion(f32[256,2,4,128]{0,3,2,1:T(8,128)S(1)} %get-tuple-element.235, bf16[2,256,2,4,128]{1,4,3,2,0:T(8,128)(2,1)} %fusion.46, f32[256,2,4]{0,2,1:T(4,128)S(1)} %get-tuple-element.217, f32[256,2,4]{0,2,1:T(4,128)S(1)} %get-tuple-element.218, f32[256,2,4]{0,2,1:T(4,128)S(1)} %get-tuple-element.219, ...), kind=kLoop, calls=%fused_computation.10.clone.1 | loop fusion | flops 2359296 | bytes 3178497 | tf_op jit(solution)/shard_map/while/body/eval_jaxpr/add | solution.py:50
  54.9 1.0 %copy.39 = bf16[256,1024]{1,0:T(8,128)(2,1)} copy(bf16[256,1024]{0,1:T(8,128)(2,1)S(1)} %bitcast.98) | data formatting | bytes 1048576 | tf_op jit(solution)/shard_map/convert_element_type | solution.py:94
  (30 shorter events, 0.7 us)
Async XLA Ops:
  0.0 33.5 %copy-start = (bf16[256,256]{1,0:T(8,128)(2,1)S(1)}, bf16[256,256]{1,0:T(8,128)(2,1)}, u32[]{:S(2)}) copy-start(bf16[256,256]{1,0:T(8,128)(2,1)} %param.7) | copy-start | bytes 393220
  0.0 19.9 %collective-permute-start = (bf16[256,256]{1,0:T(8,128)(2,1)}, bf16[256,256]{1,0:T(8,128)(2,1)S(1)}, u32[]{:S(2)}, u32[]{:S(2)}) collective-permute-start(bf16[256,256]{1,0:T(8,128)(2,1)} %param.7), channel_id=1, source_target_pairs={{0,4},{4,8},{8,12},{12,0},{1,5},{5,9},{9,13},{13,1},{2,6},{6,10},{... | collective-permute-start | bytes 393224 | tf_op jit(solution)/shard_map/ppermute | solution.py:71
  19.9 6.8 %collective-permute-start.1 = (bf16[256,256]{1,0:T(8,128)(2,1)S(1)}, bf16[256,256]{1,0:T(8,128)(2,1)S(1)}, u32[]{:S(2)}, u32[]{:S(2)}) collective-permute-start(bf16[256,256]{1,0:T(8,128)(2,1)S(1)} %collective-permute-done), channel_id=1, source_target_pairs={{0,4},{4,8},{8,12},{12,0},{1,5},{5,9},{9,13},{13,1},{2,6},{6,10},{... | collective-permute-start | bytes 393224 | tf_op jit(solution)/shard_map/ppermute | solution.py:71
  26.7 6.8 %collective-permute-start.2 = (bf16[256,256]{1,0:T(8,128)(2,1)S(1)}, bf16[256,256]{1,0:T(8,128)(2,1)S(1)}, u32[]{:S(2)}, u32[]{:S(2)}) collective-permute-start(bf16[256,256]{1,0:T(8,128)(2,1)S(1)} %collective-permute-done.1), channel_id=1, source_target_pairs={{0,4},{4,8},{8,12},{12,0},{1,5},{5,9},{9,13},{13,1},{2,6},{6,10},{... | collective-permute-start | bytes 393224 | tf_op jit(solution)/shard_map/ppermute | solution.py:71
